TPU v7x, 16 devices: a 4x2x1 block of a 4x4x8 slice. The times are simulated.
16 devices in a mesh: dp: 2 (over y, z), tp: 8 (over x, core).
Axes of the slice: x: 4, y: 2, z: 1, core: 2. Of those that a mesh axis runs over, the one named last changes fastest.
The devices are a block of a 4x4x8 slice.
Arguments:
- x: bfloat16 [128, 2048], P('dp'), parts along dimension 0
- k_cache: bfloat16 [128, 4096, 8, 64], P('dp', None, 'tp'), parts along dimension 0
- v_cache: bfloat16 [128, 4096, 8, 64], P('dp', None, 'tp'), parts along dimension 0
- gain_a: bfloat16 [2048], replicated
- wq: bfloat16 [2048, 2048], P(None, 'tp')
- wo: bfloat16 [2048, 2048], P('tp')
- gain_m: bfloat16 [2048], replicated
- w_gate: bfloat16 [2048, 8192], P(None, 'tp')
- w_up: bfloat16 [2048, 8192], P(None, 'tp')
- w_down: bfloat16 [8192, 2048], P('tp')
Outputs:
- output: bfloat16 [128, 2048], P('dp'), parts along dimension 0
There are 2 independent parts. A program takes and returns all parts, laid end to end along the dimension named above; an argument that names none is the same for every part.
All inputs are finite; a program needn't handle non-finite values.
Results may differ from a plain program's by a relative error of at most 0.017.
Values are sent between devices in bfloat16 or wider.
A program may use at most 768 MiB of HBM per device.

v0:
```python
import jax
import jax.numpy as jnp
from jax import lax
from jax.sharding import PartitionSpec as P

HEAD = 64
THETA = 10000


def normed(x, gain):
    wide = x.astype(jnp.float32)
    scale = lax.rsqrt(jnp.mean(wide * wide, -1, keepdims=True) + 1e-6)
    return (wide * scale * gain.astype(jnp.float32)).astype(jnp.bfloat16)


def turned(t, place, theta):
    half = t.shape[-1] // 2
    angle = place.astype(jnp.float32)[:, None] * theta ** (-jnp.arange(half, dtype=jnp.float32) / half)
    cos, sin = jnp.cos(angle)[:, None], jnp.sin(angle)[:, None]
    a, b = t[..., :half].astype(jnp.float32), t[..., half:].astype(jnp.float32)
    return jnp.concatenate([a * cos - b * sin, b * cos + a * sin], -1).astype(jnp.bfloat16)


def matmul(a, w):
    return jnp.dot(a, w, preferred_element_type=jnp.float32).astype(jnp.bfloat16)


def einsum(form, a, b):
    return jnp.einsum(form, a.astype(jnp.float32), b.astype(jnp.float32))


def seen_by(a, wq, k_cache, v_cache, head, theta):
    batch, cache, kv_heads = k_cache.shape[:3]
    place = jnp.full((batch,), cache - 1)
    q = turned(matmul(a, wq).reshape(batch, -1, head), place, theta).reshape(batch, kv_heads, -1, head)
    scores = einsum("bgsd,bugd->bgsu", q, k_cache) * head**-0.5
    weights = jax.nn.softmax(scores, -1).astype(jnp.bfloat16)
    return einsum("bgsu,bugd->bgsd", weights, v_cache).astype(jnp.bfloat16).reshape(batch, -1)


def hidden_of(b, w_gate, w_up):
    gate = jnp.dot(b, w_gate, preferred_element_type=jnp.float32)
    up = jnp.dot(b, w_up, preferred_element_type=jnp.float32)
    return (jax.nn.silu(gate) * up).astype(jnp.bfloat16)


def solution(mesh):
    def added(t, term):
        return (t.astype(jnp.float32) + lax.psum(term.astype(jnp.bfloat16), "tp").astype(jnp.float32)).astype(jnp.bfloat16)

    def step(x, k_cache, v_cache, gain_a, wq, wo, gain_m, w_gate, w_up, w_down):
        seen = seen_by(normed(x, gain_a), wq, k_cache, v_cache, HEAD, THETA)
        h = added(x, jnp.dot(seen, wo, preferred_element_type=jnp.float32))
        return added(h, jnp.dot(hidden_of(normed(h, gain_m), w_gate, w_up), w_down, preferred_element_type=jnp.float32))

    states, cache, columns, rows_of = P("dp", None), P("dp", None, "tp", None), P(None, "tp"), P("tp", None)
    return jax.shard_map(
        step,
        mesh=mesh,
        in_specs=(states, cache, cache, P(None), columns, rows_of, P(None), columns, columns, rows_of),
        out_specs=states,
        check_vma=False,
    )
```

profile of v0, /device:TPU:113, one launch (start us, length us, event | category | flops | bytes accessed | tf_op | source)
XLA Modules:
  0.0 165.6 jit_solution(4740565530018732801)
XLA Ops:
  6.5 0.0 copy-start
  6.6 0.0 all-reduce.3.cloned.1.call-start
  6.6 0.8 convert_element_type.66
  7.4 1.1 fusion.15
  8.5 1.7 %convolution_convert_fusion.2 = bf16[64,256]{1,0:T(8,128)(2,1)S(1)} fusion(bf16[2048,256]{1,0:T(8,128)(2,1)} %param.14, bf16[64,2048]{1,0:T(8,128)(2,1)} %param.10, f32[2048]{0:T(1024)S(1)} %convert_element_type.66, f32[64]{0:T(128)S(1)} %add_rsqrt_fusion.1), kind=kOutput, calls=%fused_computation.15 | convolution fusion | flops 67649536 | bytes 1351936 | tf_op jit(solution)/shard_map/dot_general | solution.py:25
  10.2 0.1 copy.11
  10.3 0.1 fusion.37
  10.4 0.1 copy.12
  10.5 15.1 %fusion.44 = (f32[64,4]{1,0:T(8,128)S(1)}, f32[64,4,4096]{2,1,0:T(4,128)}) fusion(bf16[64,4,64]{2,1,0:T(4,128)(2,1)S(1)} %copy.12, bf16[64,4096,1,64]{1,3,2,0:T(8,128)(2,1)} %param.11), kind=kOutput, calls=%fused_computation.54 | convolution fusion | flops 137367552 | bytes 37782528 | tf_op jit(solution)/shard_map/sub | solution.py:37
  25.7 16.0 %fusion.12 = bf16[64,4,64]{2,1,0:T(4,128)(2,1)S(1)} fusion(bf16[64,4096,1,64]{1,3,2,0:T(8,128)(2,1)} %param.12, f32[64,4,4096]{2,1,0:T(4,128)} %get-tuple-element.10, f32[64,4]{1,0:T(8,128)S(1)} %get-tuple-element.9), kind=kOutput, calls=%fused_computation.14 | convolution fusion | flops 136331264 | bytes 37782528 | tf_op jit(solution)/shard_map/bgsu,bugd->bgsd/dot_general | solution.py:29
  41.7 0.1 reshape.70
  41.8 0.0 copy-done
  41.8 1.0 convolution_convert_fusion
  42.8 0.1 all-reduce.3.cloned.1.call-update
  42.9 0.1 all-reduce.5.cloned.1.call-start
  43.0 0.0 copy-done.2
  43.0 52.8 %all-reduce.3.cloned.1.call-done = bf16[64,2048]{1,0:T(8,128)(2,1)} async-done(((bf16[64,2048]{1,0:T(8,128)(2,1)}), bf16[64,2048]{1,0:T(8,128)(2,1)}) %all-reduce.3.cloned.1.call-update) | async-done | bytes 262160 | tf_op jit(solution)/shard_map/psum | solution.py:49
  95.8 0.0 copy-done.1
  95.8 1.1 fusion.19
  97.0 3.1 %fusion.34 = f32[64,1024]{1,0:T(8,128)S(1)} fusion(bf16[2048,1024]{1,0:T(8,128)(2,1)} %param.17, bf16[64,2048]{1,0:T(8,128)(2,1)S(1)} %get-tuple-element.6, f32[2048]{0:T(1024)S(1)} %convert_element_type.77, f32[64]{0:T(128)S(1)} %add_rsqrt_fusion), kind=kOutput, calls=%fused_computation.42 | convolution fusion | flops 268959744 | bytes 4727040 | tf_op jit(solution)/shard_map/dot_general | solution.py:42
  100.1 5.8 %convolution_convert_fusion.1 = bf16[64,2048]{1,0:T(8,128)(2,1)} fusion(bf16[1024,2048]{1,0:T(8,128)(2,1)} %param.19, bf16[2048,1024]{1,0:T(8,128)(2,1)} %param.18, f32[64,1024]{1,0:T(8,128)S(1)} %fusion.34, bf16[64,2048]{1,0:T(8,128)(2,1)S(1)} %get-tuple-element.6, f32[2048]{0:T(1024)S(1)} %convert_element_type.77, f32[64]{0:T(128)S(1)} %add_rsqrt_fusion), kind=kOutput, calls=%fused_computation.10 | convolution fusion | flops 537919488 | bytes 9183488 | tf_op jit(solution)/shard_map/dot_general | solution.py:54
  105.9 0.1 all-reduce.5.cloned.1.call-update
  105.9 51.1 %all-reduce.5.cloned.1.call-done = bf16[64,2048]{1,0:T(8,128)(2,1)} async-done(((bf16[64,2048]{1,0:T(8,128)(2,1)}), bf16[64,2048]{1,0:T(8,128)(2,1)}) %all-reduce.5.cloned.1.call-update) | async-done | bytes 262160 | tf_op jit(solution)/shard_map/psum | solution.py:49
  157.0 1.7 %fusion.22 = bf16[64,2048]{1,0:T(8,128)(2,1)} fusion(bf16[64,2048]{1,0:T(8,128)(2,1)S(1)} %get-tuple-element.6, bf16[64,2048]{1,0:T(8,128)(2,1)} %all-reduce.5.cloned.1.call-done), kind=kLoop, calls=%fused_computation.29 | loop fusion | flops 524288 | bytes 786432 | tf_op jit(solution)/shard_map/convert_element_type | solution.py:49
  (7 shorter events, 0.1 us)
Async XLA Ops:
  6.5 35.3 %copy-start = (bf16[256,2048]{1,0:T(8,128)(2,1)S(1)}, bf16[256,2048]{1,0:T(8,128)(2,1)}, u32[]{:S(2)}) copy-start(bf16[256,2048]{1,0:T(8,128)(2,1)} %param.15) | copy-start | bytes 3145732
  6.6 89.2 %all-reduce.3.cloned.1.call-start = ((), (), s32[]{:S(2)}) async-start(), calls=%async_computation | async-start | bytes 524288 | tf_op jit(solution)/shard_map/psum | solution.py:49
  25.7 17.3 %copy-start.2 = (bf16[2048]{0:T(1024)(128)(2,1)S(1)}, bf16[2048]{0:T(1024)(128)(2,1)}, u32[]{:S(2)}) copy-start(bf16[2048]{0:T(1024)(128)(2,1)} %param.16) | copy-start | bytes 12292
  25.7 70.1 %copy-start.1 = (bf16[64,2048]{1,0:T(8,128)(2,1)S(1)}, bf16[64,2048]{1,0:T(8,128)(2,1)}, u32[]{:S(2)}) copy-start(bf16[64,2048]{1,0:T(8,128)(2,1)} %param.10) | copy-start | bytes 786436
  42.9 114.1 %all-reduce.5.cloned.1.call-start = ((), (), s32[]{:S(2)}) async-start(), calls=%async_computation.1 | async-start | bytes 524288 | tf_op jit(solution)/shard_map/psum | solution.py:49
Sparse Core Ops, SparseCore 0:
  43.0 52.7 all-reduce.2
  106.0 50.9 all-reduce.4
where the time goes:
time: 168 us; the launch traced here: 166 us
  waiting for transfers between devices  104 us (62%)
  matrix products  42.7 us (25%)
  between operations  13.5 us (8%)
  other arithmetic  4.9 us (3%)
    psum x2, waiting for transfers between devices, added(): lax.psum(term.astype(jnp.bfloat16), 'tp').astype(jnp.float32)  104 us
    dot_general x1, matrix products, einsum(): return jnp.einsum(form, a.astype(jnp.float32), b.astype(jnp.float32))  16 us
    sub x1, matrix products, seen_by(): weights = jax.nn.softmax(scores, -1).astype(jnp.bfloat16)  15.1 us
    dot_general x1, matrix products, step(): jnp.dot(hidden_of(normed(h, gain_m), w_gate, w_up), w_down, preferred_ele...  5.81 us
  transfers between devices with their start and end apart: 2, of which 2 were waited for; matrix products, arithmetic and copies ran while one was open for 0% of the time, Pallas kernels for 0%

commit v1 on v0

v1 whole, which is shorter than its diff:
```python
import functools

import jax
import jax.numpy as jnp
import numpy as np
from jax import lax
from jax.experimental import pallas as pl
from jax.experimental.pallas import tpu as pltpu
from jax.sharding import PartitionSpec as P

HEAD = 64
THETA = 10000
SLOTS = 8
FOUR = 4
STEP = 8
MESH = pl.DeviceIdType.MESH
ORDER = ((2, 0), (2, 1), (1, 0), (3, 0), (1, 1), (3, 1), (0, 1))
F32, BF16 = jnp.float32, jnp.bfloat16


def layer(
    chunks, x_hbm, k_hbm, v_hbm, ga_hbm, wq_hbm, wo_hbm, gm_hbm, wg_hbm, wu_hbm, wd_hbm, turn_hbm, y_hbm,
    x_ref, ga_ref, gm_ref, turn_ref, wq_ref, wo_ref, wg_ref, wu_ref, wd_ref, k_ref, v_ref, q_ref, seen_ref, a_ref, hidden_ref,
    *rest,
):
    n_chunks = len(chunks)
    own, out1, in1, h_ref, out2, in2, y_ref = (rest[i * n_chunks : (i + 1) * n_chunks] for i in range(7))
    sem, k_sem, v_sem, send_sem, recv_sem = rest[7 * n_chunks :]
    rows, d = x_ref.shape
    parts = h_ref[0].shape[0]
    part = d // parts
    groups = k_hbm.shape[0]
    me = lax.axis_index("tp")
    chip, core = me // 2, lax.rem(me, 2)

    def peer_of(ahead, other):
        return lax.rem(chip + ahead, parts // 2) * 2 + lax.rem(core + other, 2)

    def peer_from(ahead, other):
        return lax.rem(chip + parts // 2 - ahead, parts // 2) * 2 + lax.rem(core + other, 2)

    barrier = pltpu.get_barrier_semaphore()
    for ahead, other in ORDER:
        pl.semaphore_signal(barrier, inc=1, device_id={"tp": peer_of(ahead, other)}, device_id_type=MESH)

    def load(i, src, dst):
        return pltpu.make_async_copy(src, dst, sem.at[i])

    first = [load(0, x_hbm, x_ref), load(1, ga_hbm, ga_ref), load(2, turn_hbm, turn_ref), load(3, wq_hbm, wq_ref)]
    second = [load(4, wo_hbm, wo_ref), load(5, gm_hbm, gm_ref)]
    third = [load(6, wg_hbm, wg_ref), load(7, wu_hbm, wu_ref), load(8, wd_hbm, wd_ref)]

    def load_k(g, slot):
        return pltpu.make_async_copy(k_hbm.at[g], k_ref.at[slot], k_sem.at[slot])

    def load_v(g, slot):
        return pltpu.make_async_copy(v_hbm.at[g], v_ref.at[slot], v_sem.at[slot])

    for c in first:
        c.start()
    for g in range(SLOTS):
        load_k(g, g).start()
        load_v(g, g).start()
        if g == 1:
            for c in second:
                c.start()

    for c in first:
        c.wait()
    wide = x_ref[...].astype(F32)
    scale = lax.rsqrt(jnp.mean(wide * wide, -1, keepdims=True) + 1e-6)
    a = (wide * scale * ga_ref[...].astype(F32)).astype(BF16)
    q = jnp.dot(a, wq_ref[...], preferred_element_type=F32).astype(BF16).astype(F32)
    lane = lax.broadcasted_iota(jnp.int32, q.shape, 1)
    width = q.shape[1]
    swapped = jnp.where(lane % HEAD < HEAD // 2, pltpu.roll(q, width - HEAD // 2, 1), pltpu.roll(q, HEAD // 2, 1))
    q_ref[...] = (q * turn_ref[0:1, :] + swapped * turn_ref[1:2, :]).astype(BF16).astype(F32)

    lane8 = lax.broadcasted_iota(jnp.int32, (STEP, width), 1) // HEAD
    row8 = lax.broadcasted_iota(jnp.int32, (STEP, width), 0)
    low = row8 < FOUR
    zero = jnp.zeros((STEP, width), F32)

    def everywhere(t):
        t = t + pltpu.roll(t, HEAD, 1)
        return t + pltpu.roll(t, 2 * HEAD, 1)

    def spread(rep):
        halves = []
        for j in range(2):
            z = everywhere(jnp.where(lane8 == 2 * j + row8 // FOUR, rep, zero))
            halves.append(jnp.where(lane8 == row8 % FOUR, z, zero))
        return jnp.concatenate(halves, 0).astype(BF16)

    def gathered(o):
        total = zero
        for j in range(2):
            z = everywhere(jnp.where(lane8 == row8 % FOUR, o[STEP * j : STEP * (j + 1)], zero))
            total = total + jnp.where(lane8 == 2 * j + row8 // FOUR, z, zero)
        return total + pltpu.roll(total, FOUR, 0)

    def attend(i, _):
        q8 = q_ref[pl.ds(pl.multiple_of(i * STEP, STEP), STEP), :]
        turned8 = pltpu.roll(q8, FOUR, 0)
        done = []
        for half in range(2):
            g = 2 * i + half
            slot = lax.rem(g, SLOTS)
            load_k(g, slot).wait()
            load_v(g, slot).wait()
        for half in range(2):
            slot = lax.rem(2 * i + half, SLOTS)
            rep = jnp.where(low, q8, turned8) if half == 0 else jnp.where(low, turned8, q8)
            s = jnp.dot(spread(rep), k_ref[slot], preferred_element_type=F32)
            top = jnp.max(s, -1, keepdims=True)
            e = jnp.exp((s - top) * HEAD**-0.5)
            w = (e * (1.0 / jnp.sum(e, -1, keepdims=True))).astype(BF16)
            o = lax.dot_general(w, v_ref[slot], (((1,), (1,)), ((), ())), preferred_element_type=F32)
            done.append(gathered(o))
        seen_ref[pl.ds(pl.multiple_of(i * STEP, STEP), STEP), :] = jnp.where(low, done[0], done[1])
        for half in range(2):
            g = 2 * i + half

            @pl.when(g + SLOTS < groups)
            def _():
                slot = lax.rem(g, SLOTS)
                load_k(g + SLOTS, slot).start()
                load_v(g + SLOTS, slot).start()

        return 0

    def sent(c, phase, src, dst, peer):
        s = (c * 4 + phase) * parts
        return pltpu.make_async_remote_copy(
            src_ref=src, dst_ref=dst, send_sem=send_sem.at[s + peer], recv_sem=recv_sem.at[s + me], device_id={"tp": peer}, device_id_type=MESH
        )

    def got(c, phase, dst, peer):
        s = (c * 4 + phase) * parts
        pltpu.make_async_remote_copy(
            src_ref=dst, dst_ref=dst, send_sem=send_sem.at[s + peer], recv_sem=recv_sem.at[s + peer], device_id={"tp": peer}, device_id_type=MESH
        ).wait_recv()

    def cols(p):
        return pl.ds(pl.multiple_of(p * part, part), part)

    def scatter(c, phase, left, w_ref, out, into):
        for ahead, other in ORDER + ((0, 0),):
            p = peer_of(ahead, other)
            term = jnp.dot(left, w_ref[:, cols(p)], preferred_element_type=F32)
            if (ahead, other) == (0, 0):
                own[c][...] = term
            else:
                out[c][p] = term.astype(BF16)
                sent(c, phase, out[c].at[p], into[c].at[me], p).start()

    def summed(c, phase, into, residual):
        total = own[c][...]
        for ahead, other in reversed(ORDER):
            p = peer_from(ahead, other)
            got(c, phase, into[c].at[p], p)
            total = total + into[c][p].astype(F32)
        return (residual + total).astype(BF16)

    def spans(c):
        start, size = chunks[c]
        return pl.ds(start, size)

    def first_half(c):
        scatter(c, 0, seen_ref[spans(c), :].astype(BF16), wo_ref, out1, in1)

    def first_sum(c):
        h_ref[c][me] = summed(c, 0, in1, x_ref[spans(c), cols(me)].astype(F32))
        for ahead, other in ORDER:
            p = peer_of(ahead, other)
            sent(c, 1, h_ref[c].at[me], h_ref[c].at[me], p).start()

    def second_half(c):
        start, size = chunks[c]
        for ahead, other in reversed(ORDER):
            p = peer_from(ahead, other)
            got(c, 1, h_ref[c].at[p], p)
        squares = jnp.zeros((size, part), F32)
        for p in range(parts):
            wide = h_ref[c][p].astype(F32)
            squares = squares + wide * wide
        scale = lax.rsqrt(jnp.sum(squares, -1, keepdims=True) * (1.0 / d) + 1e-6)
        for p in range(parts):
            gain = gm_ref[:, p * part : (p + 1) * part].astype(F32)
            a_ref[0:size, p * part : (p + 1) * part] = (h_ref[c][p].astype(F32) * scale * gain).astype(BF16)
        tile = 256

        def unit(n, _):
            at = pl.ds(pl.multiple_of(n * tile, tile), tile)
            b = a_ref[0:size, :]
            gate = jnp.dot(b, wg_ref[:, at], preferred_element_type=F32)
            up = jnp.dot(b, wu_ref[:, at], preferred_element_type=F32)
            hidden_ref[0:size, at] = (gate * (1.0 / (1.0 + jnp.exp(-gate))) * up).astype(BF16)
            return 0

        lax.fori_loop(0, wg_ref.shape[1] // tile, unit, 0)
        scatter(c, 2, hidden_ref[0:size, :], wd_ref, out2, in2)

    def second_sum(c):
        y_ref[c][...] = summed(c, 2, in2, h_ref[c][me].astype(F32))
        at = y_hbm.at[spans(c), cols(me)]
        for ahead, other in ORDER:
            p = peer_of(ahead, other)
            sent(c, 3, y_ref[c], at, p).start()
        load(9 + c, y_ref[c], at).start()

    def last(c):
        at = y_hbm.at[spans(c), cols(me)]
        for ahead, other in reversed(ORDER):
            p = peer_from(ahead, other)
            got(c, 3, y_hbm.at[spans(c), cols(p)], p)
        load(9 + c, y_ref[c], at).wait()
        for ahead, other in ORDER:
            p = peer_of(ahead, other)
            sent(c, 0, out1[c].at[p], in1[c].at[me], p).wait_send()
            sent(c, 1, h_ref[c].at[me], h_ref[c].at[me], p).wait_send()
            sent(c, 2, out2[c].at[p], in2[c].at[me], p).wait_send()
            sent(c, 3, y_ref[c], at, p).wait_send()

    half_way = chunks[0][1] // STEP
    steps = rows // STEP
    lax.fori_loop(0, half_way, attend, 0)
    for c in second:
        c.wait()
    pl.semaphore_wait(barrier, len(ORDER))
    first_half(0)
    for c in third:
        c.start()
    lax.fori_loop(half_way, steps, attend, 0)
    first_half(1)
    first_sum(0)
    for c in third:
        c.wait()
    second_half(0)
    first_sum(1)
    second_sum(0)
    second_half(1)
    second_sum(1)
    last(0)
    last(1)


def solution(mesh):
    parts = mesh.shape["tp"]

    def step(x, k_cache, v_cache, gain_a, wq, wo, gain_m, w_gate, w_up, w_down):
        rows, d = x.shape
        seqs, places, kv_heads, head = k_cache.shape
        width = wq.shape[1]
        part = d // parts
        k, v = (jnp.transpose(t, (0, 2, 3, 1)).reshape(seqs // FOUR, FOUR * kv_heads * head, places) for t in (k_cache, v_cache))
        half = head // 2
        angle = np.float32(places - 1) * np.float32(THETA) ** (-np.arange(half, dtype=np.float32) / np.float32(half))
        angle = angle.astype(np.float32)
        cos, sin = np.cos(angle).astype(np.float32), np.sin(angle).astype(np.float32)
        turn = np.stack([np.tile(cos, width // half), np.tile(np.concatenate([-sin, sin]), width // head)])
        late = 2 * STEP
        chunks = ((0, rows - late), (rows - late, late))
        sizes = [size for _, size in chunks]
        scratch = [
            pltpu.VMEM(x.shape, BF16),
            pltpu.VMEM((1, d), BF16),
            pltpu.VMEM((1, d), BF16),
            pltpu.VMEM(turn.shape, F32),
            *[pltpu.VMEM(w.shape, BF16) for w in (wq, wo, w_gate, w_up, w_down)],
            pltpu.VMEM((SLOTS,) + k.shape[1:], BF16),
            pltpu.VMEM((SLOTS,) + v.shape[1:], BF16),
            pltpu.VMEM((rows, width), F32),
            pltpu.VMEM((rows, width), F32),
            pltpu.VMEM((max(sizes), d), BF16),
            pltpu.VMEM((max(sizes), w_gate.shape[1]), BF16),
        ]
        scratch += [pltpu.VMEM((size, part), F32) for size in sizes]
        for _ in range(5):
            scratch += [pltpu.VMEM((parts, size, part), BF16) for size in sizes]
        scratch += [pltpu.VMEM((size, part), BF16) for size in sizes]
        scratch += [
            pltpu.SemaphoreType.DMA((9 + len(chunks),)),
            pltpu.SemaphoreType.DMA((SLOTS,)),
            pltpu.SemaphoreType.DMA((SLOTS,)),
            pltpu.SemaphoreType.DMA((len(chunks) * 4 * parts,)),
            pltpu.SemaphoreType.DMA((len(chunks) * 4 * parts,)),
        ]
        return pl.pallas_call(
            functools.partial(layer, chunks),
            out_shape=jax.ShapeDtypeStruct(x.shape, BF16),
            in_specs=[pl.BlockSpec(memory_space=pl.ANY)] * 11,
            out_specs=pl.BlockSpec(memory_space=pl.ANY),
            scratch_shapes=scratch,
            compiler_params=pltpu.CompilerParams(collective_id=0, has_side_effects=True, vmem_limit_bytes=64 * 1024 * 1024 - 65536),
            name="layer",
        )(x, k, v, gain_a.reshape(1, -1), wq, wo, gain_m.reshape(1, -1), w_gate, w_up, w_down, jnp.asarray(turn))

    states, cache, columns, rows_of = P("dp", None), P("dp", None, "tp", None), P(None, "tp"), P("tp", None)
    return jax.shard_map(
        step,
        mesh=mesh,
        in_specs=(states, cache, cache, P(None), columns, rows_of, P(None), columns, columns, rows_of),
        out_specs=states,
        check_vma=False,
    )
```

time: 168 us -> 58.3 us (0.35); the launches traced: 166 us -> 58.1 us
  waiting for transfers between devices: 104 us -> 0 us
  Pallas kernels: 0 us -> 53.8 us
  matrix products: 42.7 us -> 0 us
  between operations: 13.5 us -> 0.01 us
  other arithmetic: 4.9 us -> 0 us
  local copies, waits for them, and re-layouts: 0.35 us -> 4.24 us
    psum x2 -> x0, waiting for transfers between devices: 104 us -> none  [added(): lax.psum(term.astype(jnp.bfloat16), 'tp').astype(jnp.float32)]
    pallas_call x0 -> x1, Pallas kernels: none -> 53.8 us  [step(): pl.pallas_call(functools.partial(layer, chunks), out_shape=jax.ShapeDtype...]
    dot_general x5 -> x0, matrix products: 27.6 us -> none  [the longest x1 16 us: einsum(): return jnp.einsum(form, a.astype(jnp.float32), b.astype(jnp.float32))]
    sub x1 -> x0, matrix products: 15.1 us -> none  [seen_by(): weights = jax.nn.softmax(scores, -1).astype(jnp.bfloat16)]
    convert_element_type x3 -> x0, other arithmetic: 2.49 us -> none  [the longest x1 1.71 us: added(): (t.astype(jnp.float32) + lax.psum(term.astype(jnp.bfloat16), 'tp').astype...]
    reshape x1 -> x2, local copies, waits for them, and re-layouts: 0.11 us -> 2.57 us  [the longest x1 1.29 us: step(): gain_a.reshape(1, -1)]
    reduce_sum x2 -> x0, other arithmetic: 2.24 us -> none  [normed(): scale = lax.rsqrt(jnp.mean(wide * wide, -1, keepdims=True) + 1e-06)]
  transfers between devices with their start and end apart: 2 -> 0, of which waited for: 2 -> 0; matrix products, arithmetic and copies ran while one was open for 0% -> 0% of each run, Pallas kernels for 0% -> 0%
where the time goes in v1:
time: 58.3 us; the launch traced here: 58.1 us
  Pallas kernels  53.8 us (92%)
  local copies, waits for them, and re-layouts  4.24 us (7%)
    pallas_call x1, Pallas kernels, step(): pl.pallas_call(functools.partial(layer, chunks), out_shape=jax.ShapeDtype...  53.8 us
    unnamed x1, local copies, waits for them, and re-layouts  1.67 us
    reshape x1, local copies, waits for them, and re-layouts, step(): gain_a.reshape(1, -1)  1.29 us
    reshape x1, local copies, waits for them, and re-layouts, step(): gain_m.reshape(1, -1)  1.28 us

profile of v1, /device:TPU:113, one launch (start us, length us, event | category | flops | bytes accessed | tf_op | source)
XLA Modules:
  0.0 58.1 jit_solution(3291057960487581083)
XLA Ops:
  0.0 1.3 %reshape.14.ga_hbm = bf16[1,2048]{1,0:T(2,128)(2,1)} reshape(bf16[2048]{0:T(1024)(128)(2,1)} %param.14) | data formatting | bytes 8192 | tf_op jit(solution)/shard_map/reshape | solution.py:297
  1.3 1.3 %reshape.15.gm_hbm = bf16[1,2048]{1,0:T(2,128)(2,1)} reshape(bf16[2048]{0:T(1024)(128)(2,1)} %param.17) | data formatting | bytes 8192 | tf_op jit(solution)/shard_map/reshape | solution.py:297
  2.6 53.8 %layer.1 = bf16[64,2048]{1,0:T(8,128)(2,1)} custom-call(bf16[64,2048]{1,0:T(8,128)(2,1)} %x_hbm.1, bf16[16,256,4096]{2,1,0:T(8,128)(2,1)} %bitcast.6, bf16[16,256,4096]{2,1,0:T(8,128)(2,1)} %bitcast.7, bf16[1,2048]{1,0:T(2,128)(2,1)} %reshape.14.ga_hbm, bf16[2048,256]{1,0:T(8,128)(2,1)} %wq_hbm.1, bf16[256,2048]{1,0:T(8,128)(2,1)} %wo_hbm.1, ...), custom_call_target="tpu_custom_call" | custom-call | tf_op jit(solution)/shard_map/layer/pallas_call | solution.py:289
  56.4 1.7 %copy.13 = bf16[64,2048]{1,0:T(8,128)(2,1)} copy(bf16[64,2048]{1,0:T(8,128)(2,1)} %layer.1) | data formatting | bytes 524288

commit v2 on v1

v2 whole, which is shorter than its diff:
```python
import functools

import jax
import jax.numpy as jnp
import numpy as np
from jax import lax
from jax.experimental import pallas as pl
from jax.experimental.pallas import tpu as pltpu
from jax.sharding import PartitionSpec as P

HEAD = 64
THETA = 10000
SLOTS = 6
AHEAD = 2
FOUR = 4
STEP = 8
MESH = pl.DeviceIdType.MESH
ORDER = ((2, 0), (2, 1), (1, 0), (3, 0), (1, 1), (3, 1), (0, 1))
HERE = ((0, 0),)
F32, BF16 = jnp.float32, jnp.bfloat16


def layer(
    chunks, x_hbm, k_hbm, v_hbm, ga_hbm, wq_hbm, wo_hbm, gm_hbm, wg_hbm, wu_hbm, wd_hbm, turn_hbm, y_ref,
    x_ref, ga_ref, gm_ref, turn_ref, wq_ref, wo_ref, wg_ref, wu_ref, wd_ref, k_ref, v_ref, w_ref, q_ref, seen_ref, a_ref, hidden_ref,
    *rest,
):
    n_chunks = len(chunks)
    own, out1, in1, h_ref, out2, in2 = (rest[i * n_chunks : (i + 1) * n_chunks] for i in range(6))
    sem, k_sem, v_sem, send_sem, recv_sem = rest[6 * n_chunks :]
    rows, d = x_ref.shape
    parts = h_ref[0].shape[0]
    part = d // parts
    groups = k_hbm.shape[0]
    me = lax.axis_index("tp")
    chip, core = me // 2, lax.rem(me, 2)

    def peer_of(ahead, other):
        return lax.rem(chip + ahead, parts // 2) * 2 + lax.rem(core + other, 2)

    def peer_from(ahead, other):
        return lax.rem(chip + parts // 2 - ahead, parts // 2) * 2 + lax.rem(core + other, 2)

    barrier = pltpu.get_barrier_semaphore()
    for ahead, other in ORDER:
        pl.semaphore_signal(barrier, inc=1, device_id={"tp": peer_of(ahead, other)}, device_id_type=MESH)

    def load(i, src, dst):
        return pltpu.make_async_copy(src, dst, sem.at[i])

    first = [load(0, x_hbm, x_ref), load(1, ga_hbm, ga_ref), load(2, turn_hbm, turn_ref), load(3, wq_hbm, wq_ref)]
    second = [load(4, wo_hbm, wo_ref), load(5, gm_hbm, gm_ref)]
    third = [load(6, wg_hbm, wg_ref), load(7, wu_hbm, wu_ref), load(8, wd_hbm, wd_ref)]

    def load_k(g):
        slot = lax.rem(g, SLOTS)
        return pltpu.make_async_copy(k_hbm.at[g], k_ref.at[slot], k_sem.at[slot])

    def load_v(g):
        slot = lax.rem(g, SLOTS)
        return pltpu.make_async_copy(v_hbm.at[g], v_ref.at[slot], v_sem.at[slot])

    for c in first:
        c.start()
    for c in (load_k(0), load_k(1), load_v(0)):
        c.start()

    with jax.named_scope("wait_x"):
        for c in first:
            c.wait()
    load_v(1).start()
    for g in range(2, 2 * AHEAD):
        load_k(g).start()
        load_v(g).start()
    for c in second:
        c.start()
    wide = x_ref[...].astype(F32)
    scale = lax.rsqrt(jnp.mean(wide * wide, -1, keepdims=True) + 1e-6)
    a = (wide * scale * ga_ref[...].astype(F32).reshape(1, d)).astype(BF16)
    q = jnp.dot(a, wq_ref[...], preferred_element_type=F32).astype(BF16).astype(F32)
    lane = lax.broadcasted_iota(jnp.int32, q.shape, 1)
    width = q.shape[1]
    swapped = jnp.where(lane % HEAD < HEAD // 2, pltpu.roll(q, width - HEAD // 2, 1), pltpu.roll(q, HEAD // 2, 1))
    q_ref[...] = (q * turn_ref[0:1, :] + swapped * turn_ref[1:2, :]).astype(BF16).astype(F32)

    lane8 = lax.broadcasted_iota(jnp.int32, (STEP, width), 1) // HEAD
    row8 = lax.broadcasted_iota(jnp.int32, (STEP, width), 0)
    low = row8 < FOUR
    zero = jnp.zeros((STEP, width), F32)

    def everywhere(t):
        t = t + pltpu.roll(t, HEAD, 1)
        return t + pltpu.roll(t, 2 * HEAD, 1)

    def spread(rep):
        halves = []
        for j in range(2):
            z = everywhere(jnp.where(lane8 == 2 * j + row8 // FOUR, rep, zero))
            halves.append(jnp.where(lane8 == row8 % FOUR, z, zero))
        return jnp.concatenate(halves, 0).astype(BF16)

    def gathered(o):
        total = zero
        for j in range(2):
            z = everywhere(jnp.where(lane8 == row8 % FOUR, o[STEP * j : STEP * (j + 1)], zero))
            total = total + jnp.where(lane8 == 2 * j + row8 // FOUR, z, zero)
        return total + pltpu.roll(total, FOUR, 0)

    def scores(i, half, q8):
        turned8 = pltpu.roll(q8, FOUR, 0)
        rep = jnp.where(low, q8, turned8) if half == 0 else jnp.where(low, turned8, q8)
        s = jnp.dot(spread(rep), k_ref[lax.rem(2 * i + half, SLOTS)], preferred_element_type=F32)
        top = jnp.max(s, -1, keepdims=True)
        e = jnp.exp((s - top) * HEAD**-0.5)
        return (e * (1.0 / jnp.sum(e, -1, keepdims=True))).astype(BF16)

    def values(i, half, w):
        v = v_ref[lax.rem(2 * i + half, SLOTS)]
        return gathered(lax.dot_general(w, v, (((1,), (1,)), ((), ())), preferred_element_type=F32))

    def eight(i):
        return pl.ds(pl.multiple_of(i * STEP, STEP), STEP)

    def ahead_of(i):
        for half in range(2):
            g = 2 * (i + AHEAD) + half

            @pl.when(g < groups)
            def _():
                load_k(g).start()
                load_v(g).start()

    def wait_k(i):
        with jax.named_scope("wait_k"):
            for half in range(2):
                load_k(2 * i + half).wait()

    def wait_v(i):
        with jax.named_scope("wait_v"):
            for half in range(2):
                load_v(2 * i + half).wait()

    def attend(i, _):
        ahead_of(i)
        wait_k(i)
        wait_v(i)
        q8 = q_ref[eight(i), :]
        done = [values(i, half, scores(i, half, q8)) for half in range(2)]
        seen_ref[eight(i), :] = jnp.where(low, done[0], done[1])
        return 0

    def attend_weights(i):
        ahead_of(i)
        wait_k(i)
        q8 = q_ref[eight(i), :]
        for half in range(2):
            w_ref[half] = scores(i, half, q8)

    def attend_values(i):
        wait_v(i)
        seen_ref[eight(i), :] = jnp.where(low, values(i, 0, w_ref[0]), values(i, 1, w_ref[1]))

    def sent(c, phase, src, dst, peer):
        s = (c * 4 + phase) * parts
        return pltpu.make_async_remote_copy(
            src_ref=src, dst_ref=dst, send_sem=send_sem.at[s + peer], recv_sem=recv_sem.at[s + me], device_id={"tp": peer}, device_id_type=MESH
        )

    def got(c, phase, dst, peer):
        s = (c * 4 + phase) * parts
        pltpu.make_async_remote_copy(
            src_ref=dst, dst_ref=dst, send_sem=send_sem.at[s + peer], recv_sem=recv_sem.at[s + peer], device_id={"tp": peer}, device_id_type=MESH
        ).wait_recv()

    def cols(p):
        return pl.ds(pl.multiple_of(p * part, part), part)

    def scatter(c, phase, left, w_ref, out, into, sets):
        for peers in sets:
            for ahead, other in peers:
                p = peer_of(ahead, other)
                term = jnp.dot(left, w_ref[:, cols(p)], preferred_element_type=F32)
                if (ahead, other) == (0, 0):
                    own[c][...] = term
                else:
                    out[c][p] = term.astype(BF16)
            for ahead, other in peers:
                if (ahead, other) != (0, 0):
                    p = peer_of(ahead, other)
                    sent(c, phase, out[c].at[p], into[c].at[me], p).start()

    def summed(c, phase, into, residual):
        total = own[c][...]
        for ahead, other in reversed(ORDER):
            p = peer_from(ahead, other)
            got(c, phase, into[c].at[p], p)
            total = total + into[c][p].astype(F32)
        return (residual + total).astype(BF16)

    def spans(c):
        start, size, _ = chunks[c]
        return pl.ds(start, size)

    def direct(c):
        return chunks[c][2]

    chips = parts // 2
    half_d = d // 2

    def half_of(core_):
        return pl.ds(pl.multiple_of(core_ * half_d, half_d), half_d)

    def to_other(c, phase, left, w_ref, out, into):
        p = peer_of(0, 1)
        out[c][0] = jnp.dot(left, w_ref[:, half_of(1 - core)], preferred_element_type=F32).astype(BF16)
        sent(c, phase, out[c].at[0], into[c].at[parts], p).start()
        own[c][...] = jnp.dot(left, w_ref[:, half_of(core)], preferred_element_type=F32)

    def to_all(c, phase, out, into):
        got(c, phase, into[c].at[parts], peer_of(0, 1))
        both = (own[c][...] + into[c][parts].astype(F32)).astype(BF16)
        out[c][1] = both
        into[c][core * chips + chip] = both
        for ahead, other in ORDER:
            sent(c, phase + 1, out[c].at[1], into[c].at[core * chips + chip], peer_of(ahead, other)).start()

    def from_all(c, phase, into):
        for ahead, other in ORDER:
            p = peer_from(ahead, other)
            got(c, phase + 1, into[c].at[lax.rem(p, 2) * chips + p // 2], p)

    def summed_all(c, into, residual, q):
        which, at = q * part // half_d, q * part % half_d
        total = into[c][which * chips, :, at : at + part].astype(F32)
        for p in range(1, chips):
            total = total + into[c][which * chips + p, :, at : at + part].astype(F32)
        return (residual + total).astype(BF16)

    def first_half(c):
        left = seen_ref[spans(c), :].astype(BF16)
        if direct(c):
            to_other(c, 0, left, wo_ref, out1, in1)
        else:
            scatter(c, 0, left, wo_ref, out1, in1, (ORDER + HERE,))

    def first_sum(c):
        if direct(c):
            to_all(c, 0, out1, in1)
            return
        h_ref[c][me] = summed(c, 0, in1, x_ref[spans(c), cols(me)].astype(F32))
        for ahead, other in ORDER:
            p = peer_of(ahead, other)
            sent(c, 1, h_ref[c].at[me], h_ref[c].at[me], p).start()

    def normed_first(c):
        _, size, _ = chunks[c]
        if direct(c):
            from_all(c, 0, in1)
            for p in range(parts):
                h_ref[c][p] = summed_all(c, in1, x_ref[spans(c), p * part : (p + 1) * part].astype(F32), p)
        else:
            for ahead, other in reversed(ORDER):
                p = peer_from(ahead, other)
                got(c, 1, h_ref[c].at[p], p)
        squares = jnp.zeros((size, part), F32)
        for p in range(parts):
            wide = h_ref[c][p].astype(F32)
            squares = squares + wide * wide
        scale = lax.rsqrt(jnp.sum(squares, -1, keepdims=True) * (1.0 / d) + 1e-6)
        for p in range(parts):
            gain = gm_ref[p * part : (p + 1) * part].astype(F32).reshape(1, part)
            a_ref[0:size, p * part : (p + 1) * part] = (h_ref[c][p].astype(F32) * scale * gain).astype(BF16)

    def hidden(c):
        size = chunks[c][1]
        tile = 512
        b = a_ref[0:size, :]
        for n in range(0, wg_ref.shape[1], tile):
            gate = jnp.dot(b, wg_ref[:, n : n + tile], preferred_element_type=F32)
            up = jnp.dot(b, wu_ref[:, n : n + tile], preferred_element_type=F32)
            hidden_ref[0:size, n : n + tile] = (gate * (1.0 / (1.0 + jnp.exp(-gate))) * up).astype(BF16)

    def second_half(c):
        left = hidden_ref[0 : chunks[c][1], :]
        if direct(c):
            to_other(c, 2, left, wd_ref, out2, in2)
        else:
            scatter(c, 2, left, wd_ref, out2, in2, (ORDER[:4], ORDER[4:] + HERE))

    def second_sum(c):
        if direct(c):
            to_all(c, 2, out2, in2)
            return
        at = y_ref.at[spans(c), cols(me)]
        at[...] = summed(c, 2, in2, h_ref[c][me].astype(F32))
        for ahead, other in ORDER:
            sent(c, 3, at, at, peer_of(ahead, other)).start()

    def last(c):
        if direct(c):
            from_all(c, 2, in2)
            for p in range(parts):
                y_ref[spans(c), p * part : (p + 1) * part] = summed_all(c, in2, h_ref[c][p].astype(F32), p)
            return
        for ahead, other in reversed(ORDER):
            p = peer_from(ahead, other)
            got(c, 3, y_ref.at[spans(c), cols(p)], p)

    def all_sent(c):
        at = y_ref.at[spans(c), cols(me)]
        if direct(c):
            mine = core * chips + chip
            for phase, out, into in ((0, out1, in1), (2, out2, in2)):
                sent(c, phase, out[c].at[0], into[c].at[parts], peer_of(0, 1)).wait_send()
                for ahead, other in ORDER:
                    sent(c, phase + 1, out[c].at[1], into[c].at[mine], peer_of(ahead, other)).wait_send()
            return
        for ahead, other in ORDER:
            p = peer_of(ahead, other)
            sent(c, 0, out1[c].at[p], in1[c].at[me], p).wait_send()
            sent(c, 1, h_ref[c].at[me], h_ref[c].at[me], p).wait_send()
            sent(c, 2, out2[c].at[p], in2[c].at[me], p).wait_send()
            sent(c, 3, at, at, p).wait_send()

    scope = jax.named_scope
    big, mid, late = range(3)
    ends = [(start + size) // STEP for start, size, _ in chunks]
    steps = ends[late]
    attend_weights(0)
    attend_values(0)
    lax.fori_loop(1, ends[big], attend, 0)
    with scope("wait_wo"):
        for c in second:
            c.wait()
        pl.semaphore_wait(barrier, len(ORDER))
    with scope("first0"):
        first_half(big)
    lax.fori_loop(ends[big], ends[mid], attend, 0)
    for c in third:
        c.start()
    with scope("first1"):
        first_half(mid)
    with scope("sum0"):
        first_sum(big)
    attend_weights(steps - 1)
    attend_values(steps - 1)
    with scope("first2"):
        first_half(late)
    with scope("sum1"):
        first_sum(mid)
    with scope("sum2"):
        first_sum(late)
    with scope("norm0"):
        normed_first(big)
    with scope("wait_w"):
        for c in third:
            c.wait()
    with scope("hidden0"):
        hidden(big)
    with scope("second0"):
        second_half(big)
    with scope("norm1"):
        normed_first(mid)
    with scope("hidden1"):
        hidden(mid)
    with scope("second1"):
        second_half(mid)
    with scope("norm2"):
        normed_first(late)
    with scope("hidden2"):
        hidden(late)
    with scope("second2"):
        second_half(late)
    with scope("ysum0"):
        second_sum(big)
    with scope("ysum2"):
        second_sum(late)
    with scope("ysum1"):
        second_sum(mid)
    with scope("last0"):
        last(big)
    with scope("last1"):
        last(mid)
    with scope("last2"):
        last(late)
    with scope("sent"):
        for c in range(n_chunks):
            all_sent(c)


def solution(mesh):
    parts = mesh.shape["tp"]

    def step(x, k_cache, v_cache, gain_a, wq, wo, gain_m, w_gate, w_up, w_down):
        rows, d = x.shape
        seqs, places, kv_heads, head = k_cache.shape
        width = wq.shape[1]
        part = d // parts
        k, v = (jnp.transpose(t, (0, 2, 3, 1)).reshape(seqs // FOUR, FOUR * kv_heads * head, places) for t in (k_cache, v_cache))
        half = head // 2
        angle = np.float32(places - 1) * np.float32(THETA) ** (-np.arange(half, dtype=np.float32) / np.float32(half))
        angle = angle.astype(np.float32)
        cos, sin = np.cos(angle).astype(np.float32), np.sin(angle).astype(np.float32)
        turn = np.stack([np.tile(cos, width // half), np.tile(np.concatenate([-sin, sin]), width // head)])
        mid, late = 2 * STEP, STEP
        big = rows - mid - late
        chunks = ((0, big, False), (big, mid, False), (big + mid, late, True))
        sizes = [size for _, size, _ in chunks]
        scratch = [
            pltpu.VMEM(x.shape, BF16),
            pltpu.VMEM((d,), BF16),
            pltpu.VMEM((d,), BF16),
            pltpu.VMEM(turn.shape, F32),
            *[pltpu.VMEM(w.shape, BF16) for w in (wq, wo, w_gate, w_up, w_down)],
            pltpu.VMEM((SLOTS,) + k.shape[1:], BF16),
            pltpu.VMEM((SLOTS,) + v.shape[1:], BF16),
            pltpu.VMEM((2, FOUR * width // head, places), BF16),
            pltpu.VMEM((rows, width), F32),
            pltpu.VMEM((rows, width), F32),
            pltpu.VMEM((max(sizes), d), BF16),
            pltpu.VMEM((max(sizes), w_gate.shape[1]), BF16),
        ]
        scratch += [pltpu.VMEM((size, d // 2 if whole else part), F32) for _, size, whole in chunks]
        blocks = [pltpu.VMEM((parts, size, part), BF16) for size in sizes]
        outs = [pltpu.VMEM((2, size, d // 2) if whole else (parts, size, part), BF16) for _, size, whole in chunks]
        ins = [pltpu.VMEM((parts + 1, size, d // 2) if whole else (parts, size, part), BF16) for _, size, whole in chunks]
        scratch += outs + ins + blocks + outs + ins
        scratch += [
            pltpu.SemaphoreType.DMA((9,)),
            pltpu.SemaphoreType.DMA((SLOTS,)),
            pltpu.SemaphoreType.DMA((SLOTS,)),
            pltpu.SemaphoreType.DMA((len(chunks) * 4 * parts,)),
            pltpu.SemaphoreType.DMA((len(chunks) * 4 * parts,)),
        ]
        return pl.pallas_call(
            functools.partial(layer, chunks),
            out_shape=pltpu.VMEM(x.shape, BF16),
            in_specs=[pl.BlockSpec(memory_space=pl.ANY)] * 11,
            out_specs=pl.BlockSpec(memory_space=pltpu.VMEM),
            scratch_shapes=scratch,
            compiler_params=pltpu.CompilerParams(collective_id=0, has_side_effects=True, vmem_limit_bytes=60 * 1024 * 1024),
            name="layer",
        )(x, k, v, gain_a, wq, wo, gain_m, w_gate, w_up, w_down, jnp.asarray(turn))

    states, cache, columns, rows_of = P("dp", None), P("dp", None, "tp", None), P(None, "tp"), P("tp", None)
    return jax.shard_map(
        step,
        mesh=mesh,
        in_specs=(states, cache, cache, P(None), columns, rows_of, P(None), columns, columns, rows_of),
        out_specs=states,
        check_vma=False,
    )
```

time: 58.3 us -> 44.3 us (0.76)
  Pallas kernels: 53.8 us -> 43.5 us
  local copies, waits for them, and re-layouts: 4.24 us -> 0.71 us
    pallas_call x1, Pallas kernels: 53.8 us -> 43.5 us  [step(): pl.pallas_call(functools.partial(layer, chunks), out_shape=pltpu.VMEM(x.s...]
    reshape x2 -> x0, local copies, waits for them, and re-layouts: 2.57 us -> none  [the longest x1 1.29 us: step(): gain_a.reshape(1, -1)]
    unnamed x1, local copies, waits for them, and re-layouts: 1.67 us -> 0.71 us
where the time goes in v2:
time: 44.3 us; the launch traced here: 44.2 us
  Pallas kernels  43.5 us (98%)
  local copies, waits for them, and re-layouts  0.71 us (2%)
    pallas_call x1, Pallas kernels, step(): pl.pallas_call(functools.partial(layer, chunks), out_shape=pltpu.VMEM(x.s...  43.5 us

profile of v2, /device:TPU:113, one launch (start us, length us, event | category | flops | bytes accessed | tf_op | source)
XLA Modules:
  0.0 44.2 jit_solution(4020371480360535874)
XLA Ops:
  0.0 43.5 %layer.1 = bf16[64,2048]{1,0:T(8,128)(2,1)S(1)} custom-call(bf16[64,2048]{1,0:T(8,128)(2,1)} %x_hbm.1, bf16[16,256,4096]{2,1,0:T(8,128)(2,1)} %bitcast.6, bf16[16,256,4096]{2,1,0:T(8,128)(2,1)} %bitcast.7, bf16[2048]{0:T(1024)(128)(2,1)} %ga_hbm.1, bf16[2048,256]{1,0:T(8,128)(2,1)} %wq_hbm.1, bf16[256,2048]{1,0:T(8,128)(2,1)} %wo_hbm.1, ...), custom_call_target="tpu_custom_call" | custom-call | tf_op jit(solution)/shard_map/layer/pallas_call | solution.py:435
  43.5 0.7 %copy.13 = bf16[64,2048]{1,0:T(8,128)(2,1)} copy(bf16[64,2048]{1,0:T(8,128)(2,1)S(1)} %layer.1) | data formatting | bytes 524288

commit v3 on v2

v3 whole, which is shorter than its diff:
```python
import functools

import jax
import jax.numpy as jnp
import numpy as np
from jax import lax
from jax.experimental import pallas as pl
from jax.experimental.pallas import tpu as pltpu
from jax.sharding import PartitionSpec as P

HEAD = 64
THETA = 10000
SLOTS = 3
DEPTH = 4
FOUR = 4
STEP = 8
MESH = pl.DeviceIdType.MESH
ORDER = ((2, 0), (2, 1), (1, 0), (3, 0), (1, 1), (3, 1), (0, 1))
HERE = ((0, 0),)
F32, BF16 = jnp.float32, jnp.bfloat16


def layer(
    pieces, chunks, x_hbm, k_hbm, v_hbm, ga_hbm, wq_hbm, wo_hbm, gm_hbm, wg_hbm, wu_hbm, wd_hbm, turn_hbm, y_ref,
    x_ref, ga_ref, gm_ref, turn_ref, wq_ref, wo_ref, wg_ref, wu_ref, wd_ref, k_ref, v_ref, w_ref, q_ref, seen_ref, a_ref, hidden_ref,
    *rest,
):
    counts = (len(pieces),) * 3 + (len(chunks),) * 4
    starts = [sum(counts[:n]) for n in range(len(counts) + 1)]
    own1, out1, in1, h_ref, own2, out2, in2 = (rest[a:b] for a, b in zip(starts, starts[1:]))
    sem, k_sem, v_sem, send_sem, recv_sem = rest[starts[-1] :]
    rows, d = x_ref.shape
    parts = h_ref[0].shape[0]
    part = d // parts
    me = lax.axis_index("tp")
    chip, core = me // 2, lax.rem(me, 2)

    def peer_of(ahead, other):
        return lax.rem(chip + ahead, parts // 2) * 2 + lax.rem(core + other, 2)

    barrier = pltpu.get_barrier_semaphore()
    for ahead, other in ORDER:
        pl.semaphore_signal(barrier, inc=1, device_id={"tp": peer_of(ahead, other)}, device_id_type=MESH)

    def load_at(i, src, dst):
        return pltpu.make_async_copy(src, dst, sem.at[i])

    first = [load_at(0, x_hbm, x_ref), load_at(1, ga_hbm, ga_ref), load_at(2, turn_hbm, turn_ref), load_at(3, wq_hbm, wq_ref)]
    second = [load_at(4, wo_hbm, wo_ref), load_at(5, gm_hbm, gm_ref)]
    third = [load_at(6, wg_hbm, wg_ref), load_at(7, wu_hbm, wu_ref), load_at(8, wd_hbm, wd_ref)]

    def load(hbm, ref, sem, step, half=None):
        slot = lax.rem(step, SLOTS)
        if half is None:
            return pltpu.make_async_copy(hbm.at[pl.ds(2 * step, 2)], ref.at[slot], sem.at[slot])
        return pltpu.make_async_copy(hbm.at[2 * step + half], ref.at[slot, half], sem.at[slot])

    def keys(step, half=None):
        return load(k_hbm, k_ref, k_sem, step, half)

    def values_of(step):
        return load(v_hbm, v_ref, v_sem, step)

    for c in first:
        c.start()
    keys(0, 0).start()

    with jax.named_scope("wait_x"):
        for c in first[:3]:
            c.wait()
        keys(0, 1).start()
        values_of(0).start()
        for c in first[3:]:
            c.wait()
    for n in range(2, DEPTH):
        (values_of if n % 2 else keys)(n // 2).start()
    wide = x_ref[...].astype(F32)
    scale = lax.rsqrt(jnp.mean(wide * wide, -1, keepdims=True) + 1e-6)
    a = (wide * scale * ga_ref[...].astype(F32).reshape(1, d)).astype(BF16)
    q = jnp.dot(a, wq_ref[...], preferred_element_type=F32).astype(BF16).astype(F32)
    lane = lax.broadcasted_iota(jnp.int32, q.shape, 1)
    width = q.shape[1]
    swapped = jnp.where(lane % HEAD < HEAD // 2, pltpu.roll(q, width - HEAD // 2, 1), pltpu.roll(q, HEAD // 2, 1))
    q_ref[...] = (q * turn_ref[0:1, :] + swapped * turn_ref[1:2, :]).astype(BF16).astype(F32)

    lane8 = lax.broadcasted_iota(jnp.int32, (STEP, width), 1) // HEAD
    row8 = lax.broadcasted_iota(jnp.int32, (STEP, width), 0)
    low = row8 < FOUR
    zero = jnp.zeros((STEP, width), F32)

    def everywhere(t):
        t = t + pltpu.roll(t, HEAD, 1)
        return t + pltpu.roll(t, 2 * HEAD, 1)

    def spread(rep):
        halves = []
        for j in range(2):
            z = everywhere(jnp.where(lane8 == 2 * j + row8 // FOUR, rep, zero))
            halves.append(jnp.where(lane8 == row8 % FOUR, z, zero))
        return jnp.concatenate(halves, 0).astype(BF16)

    def gathered(o):
        total = zero
        for j in range(2):
            z = everywhere(jnp.where(lane8 == row8 % FOUR, o[STEP * j : STEP * (j + 1)], zero))
            total = total + jnp.where(lane8 == 2 * j + row8 // FOUR, z, zero)
        return total + pltpu.roll(total, FOUR, 0)

    def scores(i, half, q8):
        turned8 = pltpu.roll(q8, FOUR, 0)
        rep = jnp.where(low, q8, turned8) if half == 0 else jnp.where(low, turned8, q8)
        s = jnp.dot(spread(rep), k_ref[lax.rem(i, SLOTS), half], preferred_element_type=F32)
        top = jnp.max(s, -1, keepdims=True)
        e = jnp.exp((s - top) * HEAD**-0.5)
        return (e * (1.0 / jnp.sum(e, -1, keepdims=True))).astype(BF16)

    def values(i, half, w):
        v = v_ref[lax.rem(i, SLOTS), half]
        return gathered(lax.dot_general(w, v, (((1,), (1,)), ((), ())), preferred_element_type=F32))

    def eight(i):
        return pl.ds(pl.multiple_of(i * STEP, STEP), STEP)

    def start_after(step, kind):
        later = step + (kind + DEPTH) // 2

        @pl.when(later < rows // STEP)
        def _():
            (values_of if (kind + DEPTH) % 2 else keys)(later).start()

    def weigh_all(i):
        with jax.named_scope("wait_k"):
            keys(i).wait()
        start_after(i, 0)
        q8 = q_ref[eight(i), :]
        for half in range(2):
            w_ref[half] = scores(i, half, q8)

    def attend_last(i):
        with jax.named_scope("wait_v"):
            values_of(i).wait()
        start_after(i, 1)
        seen_ref[eight(i), :] = jnp.where(low, values(i, 0, w_ref[0]), values(i, 1, w_ref[1]))

    def attend(i, _):
        weigh_all(i)
        attend_last(i)
        return 0

    n_pieces = len(pieces)

    def sent(e, src, dst, peer):
        return pltpu.make_async_remote_copy(
            src_ref=src, dst_ref=dst, send_sem=send_sem.at[e], recv_sem=recv_sem.at[e], device_id={"tp": peer}, device_id_type=MESH
        )

    def got(e, all_of):
        sent(e, all_of, all_of, peer_of(0, 1)).wait_recv()

    def all_but_one(ref):
        return ref.at[pl.ds(0, parts - 1)]

    def all_but_one_part(c):
        start, size, *_ = chunks[c]
        return y_ref.at[span(start, size), pl.ds(0, d - part)]

    def cols(p):
        return pl.ds(pl.multiple_of(p * part, part), part)

    def span(start, size):
        return pl.ds(start, size)

    def scatter(e, left, w_ref, own, out, into):
        for ahead, other in ORDER + HERE:
            p = peer_of(ahead, other)
            term = jnp.dot(left, w_ref[:, cols(p)], preferred_element_type=F32)
            if (ahead, other) == (0, 0):
                own[...] = term
            else:
                out[p] = term.astype(BF16)
        for ahead, other in ORDER:
            p = peer_of(ahead, other)
            sent(e, out.at[p], into.at[me], p).start()

    def summed(e, own, into, residual):
        got(e, all_but_one(into))
        total = own[...]
        for ahead, other in ORDER:
            total = total + into[peer_of(ahead, other)].astype(F32)
        return (residual + total).astype(BF16)

    chips = parts // 2
    half_d = d // 2
    mine = core * chips + chip

    def half_of(core_):
        return pl.ds(pl.multiple_of(core_ * half_d, half_d), half_d)

    def to_other(e, left, w_ref, own, out, into):
        out[0] = jnp.dot(left, w_ref[:, half_of(1 - core)], preferred_element_type=F32).astype(BF16)
        sent(e, out.at[0], into.at[parts], peer_of(0, 1)).start()
        own[...] = jnp.dot(left, w_ref[:, half_of(core)], preferred_element_type=F32)

    def to_all(e, own, out, into):
        got(e, into.at[parts])
        both = (own[...] + into[parts].astype(F32)).astype(BF16)
        out[1] = both
        into[mine] = both
        for ahead, other in ORDER:
            sent(e + 1, out.at[1], into.at[mine], peer_of(ahead, other)).start()

    def from_all(e, into):
        got(e + 1, all_but_one(into))

    def summed_all(into, residual, q):
        which, at = q * part // half_d, q * part % half_d
        total = into[which * chips, :, at : at + part].astype(F32)
        for p in range(1, chips):
            total = total + into[which * chips + p, :, at : at + part].astype(F32)
        return (residual + total).astype(BF16)

    def first_half(i):
        start, size, whole = pieces[i]
        (to_other if whole else scatter)(2 * i, seen_ref[span(start, size), :].astype(BF16), wo_ref, own1[i], out1[i], in1[i])

    def first_sum(i):
        start, size, whole = pieces[i]
        if whole:
            to_all(2 * i, own1[i], out1[i], in1[i])
            return
        at = h_ref[i].at[me]
        at[...] = summed(2 * i, own1[i], in1[i], x_ref[span(start, size), cols(me)].astype(F32))
        for ahead, other in ORDER:
            sent(2 * i + 1, at, at, peer_of(ahead, other)).start()

    def normed_first(c):
        start, size, _, members = chunks[c]
        for i in members:
            first, count, whole = pieces[i]
            if whole:
                from_all(2 * i, in1[i])
                for p in range(parts):
                    residual = x_ref[span(first, count), p * part : (p + 1) * part].astype(F32)
                    h_ref[c][p, first - start : first - start + count, :] = summed_all(in1[i], residual, p)
            else:
                got(2 * i + 1, all_but_one(h_ref[c]))
        squares = jnp.zeros((size, part), F32)
        for p in range(parts):
            wide = h_ref[c][p].astype(F32)
            squares = squares + wide * wide
        scale = lax.rsqrt(jnp.sum(squares, -1, keepdims=True) * (1.0 / d) + 1e-6)
        for p in range(parts):
            gain = gm_ref[p * part : (p + 1) * part].astype(F32).reshape(1, part)
            a_ref[0:size, p * part : (p + 1) * part] = (h_ref[c][p].astype(F32) * scale * gain).astype(BF16)

    def hidden(c, tiles=(0, 1)):
        size = chunks[c][1]
        tile = wg_ref.shape[1] // 2
        b = a_ref[0:size, :]
        for n in (t * tile for t in tiles):
            gate = jnp.dot(b, wg_ref[:, n : n + tile], preferred_element_type=F32)
            up = jnp.dot(b, wu_ref[:, n : n + tile], preferred_element_type=F32)
            hidden_ref[0:size, n : n + tile] = (gate * (1.0 / (1.0 + jnp.exp(-gate))) * up).astype(BF16)

    def exchange(c):
        return 2 * (n_pieces + c)

    def second_half(c):
        _, size, whole, _ = chunks[c]
        (to_other if whole else scatter)(exchange(c), hidden_ref[0:size, :], wd_ref, own2[c], out2[c], in2[c])

    def second_sum(c):
        start, size, whole, _ = chunks[c]
        if whole:
            to_all(exchange(c), own2[c], out2[c], in2[c])
            return
        at = y_ref.at[span(start, size), cols(me)]
        at[...] = summed(exchange(c), own2[c], in2[c], h_ref[c][me].astype(F32))
        for ahead, other in ORDER:
            sent(exchange(c) + 1, at, at, peer_of(ahead, other)).start()

    def last(c):
        start, size, whole, _ = chunks[c]
        if whole:
            from_all(exchange(c), in2[c])
            for p in range(parts):
                y_ref[span(start, size), p * part : (p + 1) * part] = summed_all(in2[c], h_ref[c][p].astype(F32), p)
            return
        got(exchange(c) + 1, all_but_one_part(c))

    def all_sent():
        def wait(e, all_of):
            sent(e, all_of, all_of, peer_of(0, 1)).wait_send()

        for i, (_, _, whole) in enumerate(pieces):
            wait(2 * i, out1[i].at[0] if whole else all_but_one(out1[i]))
            wait(2 * i + 1, all_but_one(in1[i] if whole else h_ref[i]))
        for c, (_, _, whole, _) in enumerate(chunks):
            wait(exchange(c), out2[c].at[0] if whole else all_but_one(out2[c]))
            wait(exchange(c) + 1, all_but_one(in2[c]) if whole else all_but_one_part(c))

    scope = jax.named_scope
    steps = rows // STEP
    ends = [(start + size) // STEP for start, size, _ in pieces]
    big, mid, late = range(3)
    lax.fori_loop(0, 2, attend, 0)
    for c in second:
        c.start()
    lax.fori_loop(2, ends[0], attend, 0)
    with scope("wait_wo"):
        for c in second:
            c.wait()
        pl.semaphore_wait(barrier, len(ORDER))
    with scope("first0"):
        first_half(0)
    lax.fori_loop(ends[0], ends[1], attend, 0)
    with scope("first1"):
        first_half(1)
    with scope("sum0"):
        first_sum(0)
    weigh_all(steps - 2)
    with scope("sum1"):
        first_sum(1)
    attend_last(steps - 2)
    for c in third:
        c.start()
    with scope("first2"):
        first_half(2)
    weigh_all(steps - 1)
    with scope("sum2"):
        first_sum(2)
    attend_last(steps - 1)
    with scope("first3"):
        first_half(3)
    with scope("norm0"):
        normed_first(big)
    with scope("wait_w"):
        for c in third[:2]:
            c.wait()
    with scope("hidden0"):
        hidden(big, (0,))
    with scope("sum3"):
        first_sum(3)
    with scope("hidden0"):
        hidden(big, (1,))
    third[2].wait()
    with scope("second0"):
        second_half(big)
    with scope("norm1"):
        normed_first(mid)
    with scope("hidden1"):
        hidden(mid)
    with scope("second1"):
        second_half(mid)
    with scope("norm2"):
        normed_first(late)
    with scope("hidden2"):
        hidden(late)
    with scope("ysum0"):
        second_sum(big)
    with scope("second2"):
        second_half(late)
    with scope("ysum2"):
        second_sum(late)
    with scope("ysum1"):
        second_sum(mid)
    with scope("last2"):
        last(late)
    with scope("last3"):
        last(big)
        last(mid)
    with scope("sent"):
        all_sent()


def solution(mesh):
    parts = mesh.shape["tp"]

    def step(x, k_cache, v_cache, gain_a, wq, wo, gain_m, w_gate, w_up, w_down):
        rows, d = x.shape
        seqs, places, kv_heads, head = k_cache.shape
        width = wq.shape[1]
        part = d // parts
        k, v = (jnp.transpose(t, (0, 2, 3, 1)).reshape(seqs // FOUR, FOUR * kv_heads * head, places) for t in (k_cache, v_cache))
        half = head // 2
        angle = np.float32(places - 1) * np.float32(THETA) ** (-np.arange(half, dtype=np.float32) / np.float32(half))
        angle = angle.astype(np.float32)
        cos, sin = np.cos(angle).astype(np.float32), np.sin(angle).astype(np.float32)
        turn = np.stack([np.tile(cos, width // half), np.tile(np.concatenate([-sin, sin]), width // head)])
        pieces = ((0, rows - 4 * STEP, False), (rows - 4 * STEP, 2 * STEP, True), (rows - 2 * STEP, STEP, True), (rows - STEP, STEP, True))
        chunks = ((0, rows - 4 * STEP, False, (0,)), (rows - 4 * STEP, 3 * STEP, False, (1, 2)), (rows - STEP, STEP, True, (3,)))
        sizes = [size for _, size, *_ in chunks]
        scratch = [
            pltpu.VMEM(x.shape, BF16),
            pltpu.VMEM((d,), BF16),
            pltpu.VMEM((d,), BF16),
            pltpu.VMEM(turn.shape, F32),
            *[pltpu.VMEM(w.shape, BF16) for w in (wq, wo, w_gate, w_up, w_down)],
            pltpu.VMEM((SLOTS, 2) + k.shape[1:], BF16),
            pltpu.VMEM((SLOTS, 2) + v.shape[1:], BF16),
            pltpu.VMEM((2, FOUR * width // head, places), BF16),
            pltpu.VMEM((rows, width), F32),
            pltpu.VMEM((rows, width), F32),
            pltpu.VMEM((max(sizes), d), BF16),
            pltpu.VMEM((max(sizes), w_gate.shape[1]), BF16),
        ]

        def buffers(sums):
            each = [(size, whole) for _, size, whole, *_ in sums]
            return (
                [pltpu.VMEM((size, d // 2 if whole else part), F32) for size, whole in each]
                + [pltpu.VMEM((2, size, d // 2) if whole else (parts, size, part), BF16) for size, whole in each]
                + [pltpu.VMEM((parts + 1, size, d // 2) if whole else (parts, size, part), BF16) for size, whole in each]
            )

        scratch += buffers(pieces) + [pltpu.VMEM((parts, size, part), BF16) for size in sizes] + buffers(chunks)
        scratch += [
            pltpu.SemaphoreType.DMA((9,)),
            pltpu.SemaphoreType.DMA((SLOTS,)),
            pltpu.SemaphoreType.DMA((SLOTS,)),
            pltpu.SemaphoreType.DMA((2 * (len(pieces) + len(chunks)),)),
            pltpu.SemaphoreType.DMA((2 * (len(pieces) + len(chunks)),)),
        ]
        return pl.pallas_call(
            functools.partial(layer, pieces, chunks),
            out_shape=pltpu.VMEM(x.shape, BF16),
            in_specs=[pl.BlockSpec(memory_space=pl.ANY)] * 11,
            out_specs=pl.BlockSpec(memory_space=pltpu.VMEM),
            scratch_shapes=scratch,
            compiler_params=pltpu.CompilerParams(collective_id=0, has_side_effects=True, vmem_limit_bytes=60 * 1024 * 1024),
            name="layer",
        )(x, k, v, gain_a, wq, wo, gain_m, w_gate, w_up, w_down, jnp.asarray(turn))

    states, cache, columns, rows_of = P("dp", None), P("dp", None, "tp", None), P(None, "tp"), P("tp", None)
    return jax.shard_map(
        step,
        mesh=mesh,
        in_specs=(states, cache, cache, P(None), columns, rows_of, P(None), columns, columns, rows_of),
        out_specs=states,
        check_vma=False,
    )
```

time: 44.3 us -> 40.6 us (0.916)
  Pallas kernels: 43.5 us -> 39.8 us
    pallas_call x1, Pallas kernels: 43.5 us -> 39.8 us  [step(): pl.pallas_call(functools.partial(layer, pieces, chunks), out_shape=pltpu....]
where the time goes in v3:
time: 40.6 us; the launch traced here: 40.5 us
  Pallas kernels  39.8 us (98%)
  local copies, waits for them, and re-layouts  0.71 us (2%)
    pallas_call x1, Pallas kernels, step(): pl.pallas_call(functools.partial(layer, pieces, chunks), out_shape=pltpu....  39.8 us

profile of v3, /device:TPU:113, one launch (start us, length us, event | category | flops | bytes accessed | tf_op | source)
XLA Modules:
  0.0 40.5 jit_solution(5956803156995881851)
XLA Ops:
  0.0 39.8 %layer.1 = bf16[64,2048]{1,0:T(8,128)(2,1)S(1)} custom-call(bf16[64,2048]{1,0:T(8,128)(2,1)} %x_hbm.1, bf16[16,256,4096]{2,1,0:T(8,128)(2,1)} %bitcast.6, bf16[16,256,4096]{2,1,0:T(8,128)(2,1)} %bitcast.7, bf16[2048]{0:T(1024)(128)(2,1)} %ga_hbm.1, bf16[2048,256]{1,0:T(8,128)(2,1)} %wq_hbm.1, bf16[256,2048]{1,0:T(8,128)(2,1)} %wo_hbm.1, ...), custom_call_target="tpu_custom_call" | custom-call | tf_op jit(solution)/shard_map/layer/pallas_call | solution.py:424
  39.8 0.7 %copy.13 = bf16[64,2048]{1,0:T(8,128)(2,1)} copy(bf16[64,2048]{1,0:T(8,128)(2,1)S(1)} %layer.1) | data formatting | bytes 524288
